TPU v7x, 256 devices: a whole 4x4x8 slice. The times are simulated.
256 devices in a mesh: ens: 4 (over x), zero: 16 (over z, core), cols: 4 (over y).
Axes of the slice: x: 4, y: 4, z: 8, core: 2. Of those that a mesh axis runs over, the one named last changes fastest.
Arguments:
- one_gate: float32 [8192, 8192], P(('ens', 'zero'), 'cols'), parts along dimension 0, may hold values from -0.1875 to 0.1875
- other_gate: float32 [8192, 8192], P(('ens', 'zero'), 'cols'), parts along dimension 0, may hold values from -0.125 to 0.125
- one_up: float32 [8192, 8192], P(('ens', 'zero'), 'cols'), parts along dimension 0, may hold values from -0.1875 to 0.1875
- other_up: float32 [8192, 8192], P(('ens', 'zero'), 'cols'), parts along dimension 0, may hold values from -0.125 to 0.125
- mix_share: float32 [8192], P(('ens', 'zero')), parts along dimension 0, may hold values from 0.2 to 0.8
- norm_train: float32 [8192], P(('ens', 'zero', 'cols')), parts along dimension 0, may hold values from 0.25 to 1.75
- norm_step: float32 [8192], P(('ens', 'zero', 'cols')), parts along dimension 0, may hold values from -0.3 to 0.3
Outputs:
- serve_gate: bfloat16 [8192, 8192], P('ens', 'cols'), parts along dimension 0
- serve_up: bfloat16 [8192, 8192], P('ens', 'cols'), parts along dimension 0
- factor_gate: float32 [32768], P(('ens', 'cols')), parts along dimension 0
- factor_up: float32 [32768], P(('ens', 'cols')), parts along dimension 0
- serve_norm: bfloat16 [8192], P('ens'), parts along dimension 0
There are 4 independent parts, one for each index of `ens`. A program takes and returns all parts, laid end to end along the dimension named above; each array names one. Nothing has to cross between parts.
All inputs are finite; a program needn't handle non-finite values. Where the computation divides by a largest or mean magnitude, that divisor is 1e-20 or more.
Results may differ from a plain program's by a relative error of at most 0.001.
Values may be sent and summed in bfloat16 or wider, within the bound.
A program may use at most 128 MiB of HBM per device.

v0:
```python
import jax
import jax.numpy as jnp
from jax import lax
from jax.sharding import PartitionSpec as P

D_MODEL = 2048


def from_everyone(x, axis):
    size = lax.axis_size(axis)
    return lax.all_to_all(jnp.broadcast_to(x[None], (size, *x.shape)), axis, 0, 0, tiled=True)


def over_copies(x, axis):
    return from_everyone(x, axis).sum(axis=0)


def packed_total(arrays, axis):
    vector, at, gathered = (jnp.concatenate([a.reshape(-1) for a in arrays]), 0, [])
    running = over_copies(vector, axis)
    for a in arrays:
        gathered.append(running[at : at + a.size].reshape(a.shape))
        at += a.size
    return tuple(gathered)


def in_one_piece(arrays, axis, dim, along):
    ends, at = ([], 0)
    for a in arrays[:-1]:
        at += a.shape[along]
        ends.append(at)
    both = jnp.concatenate(arrays, axis=along)
    return tuple(jnp.split(lax.all_gather(both, axis, axis=dim, tiled=True), ends, axis=along))


def in_order(pieces, dim):
    pieces = jnp.moveaxis(pieces, 0, dim)
    lengths = pieces.shape
    return pieces.reshape(*lengths[:dim], lengths[dim] * lengths[dim + 1], *lengths[dim + 2 :])


def collect(x, axis, dim):
    pieces = from_everyone(x, axis)
    return in_order(pieces, dim)


def local(one_gate, other_gate, one_up, other_up, mix_share, norm_train, norm_step):
    fresh_gate = mix_share[:, None] * one_gate + (1.0 - mix_share[:, None]) * other_gate
    fresh_up = mix_share[:, None] * one_up + (1.0 - mix_share[:, None]) * other_up
    total_gate, total_up = packed_total(
        (jnp.sum(jnp.abs(fresh_gate), axis=0), jnp.sum(jnp.abs(fresh_up), axis=0)), "zero"
    )
    factor_gate = total_gate / D_MODEL
    factor_up = total_up / D_MODEL
    narrow_gate, narrow_up = (
        (fresh_gate / factor_gate).astype(jnp.bfloat16),
        (fresh_up / factor_up).astype(jnp.bfloat16),
    )
    serve_gate, serve_up = in_one_piece((narrow_gate, narrow_up), "zero", 0, 1)
    serve_norm = collect((norm_train + norm_step).astype(jnp.bfloat16), ("zero", "cols"), 0)
    return (serve_gate, serve_up, factor_gate, factor_up, serve_norm)


def solution(mesh):
    return jax.shard_map(
        local,
        mesh=mesh,
        in_specs=(
            P(("ens", "zero"), "cols"),
            P(("ens", "zero"), "cols"),
            P(("ens", "zero"), "cols"),
            P(("ens", "zero"), "cols"),
            P(("ens", "zero")),
            P(("ens", "zero", "cols")),
            P(("ens", "zero", "cols")),
        ),
        out_specs=(
            P("ens", "cols"),
            P("ens", "cols"),
            P(("ens", "cols")),
            P(("ens", "cols")),
            P("ens"),
        ),
        check_vma=False,
    )
```

profile of v0, /device:TPU:1, one launch (start us, length us, event | category | flops | bytes accessed | tf_op | source)
XLA Modules:
  0.0 147.9 jit_solution(4524025194384531195)
XLA Ops:
  7.2 0.0 copy-start.2
  7.2 0.0 copy-start.3
  7.2 0.0 all-gather.2.cloned.1.call-start
  7.2 0.7 broadcast_subtract_fusion
  7.9 2.8 %abs_reduce_fusion.1 = (f32[2048]{0:T(1024)S(1)}, f32[2048]{0:T(1024)S(1)}) fusion(f32[128,2048]{1,0:T(8,128)} %param.8, f32[128]{0:T(128)S(1)} %broadcast_subtract_fusion, f32[128,2048]{1,0:T(8,128)} %param.7, f32[128]{0:T(128)} %param.11, f32[128,2048]{1,0:T(8,128)} %param.10, f32[128,2048]{1,0:T(8,128)} %param.9), kind=kLoop, calls=%fused_computation.5 | loop fusion | flops 2617344 | bytes 4211712 | tf_op jit(solution)/shard_map/reduce_sum | solution.py:51
  10.7 0.2 broadcast_in_dim.4
  10.9 21.4 %all_to_all.12 = f32[16,1,4096]{2,1,0:T(1,128)S(1)} all-to-all(f32[16,1,4096]{2,1,0:T(1,128)S(1)} %broadcast_in_dim.4), channel_id=1, replica_groups=mesh['ens'=4,'zero'=16,'cols'=4] {'zero'}, dimensions={0} | all-to-all | bytes 524288 | tf_op jit(solution)/shard_map/all_to_all | solution.py:11
  32.2 0.2 reduce_sum.29
  32.4 0.0 copy-start
  32.4 0.0 copy-start.1
  32.4 2.8 %divide_convert_fusion.1 = (bf16[128,2048]{1,0:T(8,128)(2,1)S(1)}, bf16[128,2048]{1,0:T(8,128)(2,1)S(1)}) fusion(f32[2048]{0:T(1024)S(1)} %get-tuple-element.9, f32[128,2048]{1,0:T(8,128)} %param.8, f32[128]{0:T(128)S(1)} %broadcast_subtract_fusion, f32[128,2048]{1,0:T(8,128)} %param.7, f32[128]{0:T(128)} %param.11, f32[2048]{0:T(1024)S(1)} %get-tuple-element.10, ...), kind=kLoop, calls=%fused_computation.2 | loop fusion | flops 2621440 | bytes 5260288 | tf_op jit(solution)/shard_map/convert_element_type | solution.py:56
  35.2 1.0 pad_maximum_fusion
  36.3 0.0 all-gather.2.cloned.1.call-update
  36.3 0.0 copy-done.2
  36.3 0.0 copy-done.3
  36.3 15.2 %all_to_all.13 = bf16[64,1,32]{2,1,0:T(2,128)(2,1)S(1)} all-to-all(bf16[64,1,32]{2,1,0:T(2,128)(2,1)S(1)} %broadcast_in_dim.5), channel_id=1, replica_groups=mesh['ens'=4,'zero'=16,'cols'=4] {'zero','cols'}, dimensions={0} | all-to-all | bytes 8192 | tf_op jit(solution)/shard_map/all_to_all | solution.py:11
  51.5 0.1 reduce.1
  51.6 0.7 reshape.31
  52.3 76.8 %all-gather.2.cloned.1.call-done = bf16[2048,4096]{1,0:T(8,128)(2,1)} async-done(((bf16[128,4096]{1,0:T(8,128)(2,1)}), bf16[2048,4096]{1,0:T(8,128)(2,1)}) %all-gather.2.cloned.1.call-update) | async-done | bytes 16777232 | tf_op jit(solution)/shard_map/all_gather | solution.py:33
  129.1 11.9 %fusion = (bf16[2048,2048]{1,0:T(8,128)(2,1)}, bf16[2048,2048]{1,0:T(8,128)(2,1)}) fusion(bf16[2048,4096]{1,0:T(8,128)(2,1)} %all-gather.2.cloned.1.call-done), kind=kLoop, calls=%fused_computation.12 | loop fusion | bytes 33554432 | tf_op jit(solution)/shard_map/split | solution.py:33
  141.1 0.0 copy-done
  141.1 0.0 copy-done.1
  (4 shorter events, 0.0 us)
Async XLA Ops:
  7.2 29.1 %copy-start.2 = (f32[32]{0:T(128)S(1)}, f32[32]{0:T(128)}, u32[]{:S(2)}) copy-start(f32[32]{0:T(128)} %param.12) | copy-start | bytes 388
  7.2 29.1 %copy-start.3 = (f32[32]{0:T(128)S(1)}, f32[32]{0:T(128)}, u32[]{:S(2)}) copy-start(f32[32]{0:T(128)} %param.13) | copy-start | bytes 388
  7.2 121.9 %all-gather.2.cloned.1.call-start = ((), (), s32[]{:S(2)}) async-start(), calls=%async_computation.2 | async-start | bytes 17825792 | tf_op jit(solution)/shard_map/all_gather | solution.py:33
  32.4 108.7 %copy-start = (f32[2048]{0:T(1024)}, f32[2048]{0:T(1024)S(1)}, u32[]{:S(2)}) copy-start(f32[2048]{0:T(1024)S(1)} %get-tuple-element.9) | copy-start | bytes 24580
  32.4 108.7 %copy-start.1 = (f32[2048]{0:T(1024)}, f32[2048]{0:T(1024)S(1)}, u32[]{:S(2)}) copy-start(f32[2048]{0:T(1024)S(1)} %get-tuple-element.10) | copy-start | bytes 24580
Sparse Core Ops, SparseCore 0:
  36.4 92.6 all-gather.1
where the time goes:
time: 148 us
  waiting for transfers between devices  76.9 us (52%)
  blocking collectives  36.5 us (25%)
  between operations  14.1 us (10%)
  local copies, waits for them, and re-layouts  12.9 us (9%)
  other arithmetic  7.51 us (5%)
    all_gather x1, waiting for transfers between devices, in_one_piece(): lax.all_gather(both, axis, axis=dim, tiled=True)  76.8 us
    all_to_all x2, blocking collectives, from_everyone(): lax.all_to_all(jnp.broadcast_to(x[None], (size, *x.shape)), axis, 0, 0, t...  36.5 us
    split x1, local copies, waits for them, and re-layouts, in_one_piece(): jnp.split(lax.all_gather(both, axis, axis=dim, tiled=True), ends, axis=al...  11.9 us
  transfers between devices with their start and end apart: 1, of which 1 were waited for; matrix products, arithmetic and copies ran while one was open for 1% of the time, Pallas kernels for 0%

commit v1 on v0

v1 whole, which is shorter than its diff:
```python
import jax
import jax.numpy as jnp
from jax import lax
from jax.experimental import pallas as pl
from jax.experimental.pallas import tpu as pltpu
from jax.sharding import PartitionSpec as P

D_MODEL = 2048
MESH = pl.DeviceIdType.MESH
CHIPS = 8
CORES = 2
COLS = 4
PARTS = 2


def gather_kernel(
    one_gate, other_gate, one_up, other_up, mix, norm_train, norm_step,
    out, factor, norm,
    held, mix_rows, sums, paired, chip_sums, norm_cols,
    load_sem, pair_send, pair_recv, sum_send, sum_recv, fac_send, fac_recv,
    col_send, col_recv, nz_send, nz_recv, np_send, np_recv,
    ici_send, ici_recv, die_send, die_recv,
):
    zero = lax.axis_index("zero")
    y = lax.axis_index("cols")
    z, core = zero // CORES, lax.rem(zero, CORES)
    rows, columns = one_gate.shape
    partner = {"zero": z * CORES + 1 - core}
    first, second = 1 - core, core
    half = rows // 2
    size = half // PARTS

    def chip(k):
        return {"zero": lax.rem(z + k, CHIPS) * CORES + core}

    def col(k):
        return {"cols": lax.rem(y + k, COLS)}

    groups = 4
    step = rows // groups

    def load(matrix, which, g):
        source = ((one_gate, other_gate), (one_up, other_up))[matrix][which]
        at = pl.ds(g * step, step)
        return pltpu.make_async_copy(source.at[at], held.at[matrix, which, at], load_sem.at[matrix, which, g])

    def start_loads(matrix):
        for g in range(groups):
            for which in range(2):
                load(matrix, which, g).start()

    @pl.when(core == 0)
    def _():
        start_loads(1)
        start_loads(0)

    @pl.when(core == 1)
    def _():
        start_loads(0)
        start_loads(1)

    barrier = pltpu.get_barrier_semaphore()
    pl.semaphore_signal(barrier, inc=1, device_id=partner, device_id_type=MESH)
    for k in range(1, CHIPS):
        pl.semaphore_signal(barrier, inc=1, device_id=chip(k), device_id_type=MESH)
    for k in range(1, COLS):
        pl.semaphore_signal(barrier, inc=1, device_id=col(k), device_id_type=MESH)

    mix_rows[...] = jnp.broadcast_to(mix[...], (rows, rows)).T
    lane = lax.broadcasted_iota(jnp.int32, (1, 128), 1)
    gain = norm_train[...] + norm_step[...]
    width = gain.shape[1]
    gain = jnp.concatenate([gain] * COLS, axis=1)
    norm_cols[y] = jnp.where((lane >= y * width) & (lane < (y + 1) * width), gain, 0.0)

    def average(matrix):
        total = jnp.zeros((8, columns), jnp.float32)
        for g in range(groups):
            for which in range(2):
                at = pl.ds(g * step, step)
                pltpu.make_async_copy(one_gate.at[at], held.at[matrix, which, at], load_sem.at[matrix, which, g]).wait()

            def body(i, total):
                at = pl.ds(pl.multiple_of(g * step + i * 8, 8), 8)
                share = jnp.concatenate([mix_rows[at]] * (columns // 128), axis=1)
                fresh = share * held[matrix, 0, at] + (1.0 - share) * held[matrix, 1, at]
                held[matrix, 0, at] = fresh
                return total + jnp.abs(fresh)

            total = lax.fori_loop(0, step // 8, body, total)
        sums[matrix] = jnp.sum(total, axis=0, keepdims=True)

    average(first)
    pl.semaphore_wait(barrier, 1 + CHIPS - 1 + COLS - 1)
    pair = pltpu.make_async_remote_copy(
        sums.at[first], paired, pair_send, pair_recv, device_id=partner, device_id_type=MESH
    )
    pair.start()
    col_copies = [
        pltpu.make_async_remote_copy(
            norm_cols.at[y], norm_cols.at[y], col_send.at[k], col_recv.at[k], device_id=col(k), device_id_type=MESH
        )
        for k in range(1, COLS)
    ]
    for copy in col_copies:
        copy.start()
    average(second)
    pair.wait_recv()
    chip_sums[z] = sums[second] + paired[...]
    sum_copies = [
        pltpu.make_async_remote_copy(
            chip_sums.at[z], chip_sums.at[z], sum_send.at[k], sum_recv.at[k], device_id=chip(k), device_id_type=MESH
        )
        for k in (4, 3, 5, 2, 6, 1, 7)
    ]
    for copy in sum_copies:
        copy.start()

    for copy in col_copies:
        copy.wait_recv()
    norm[core, z] = norm_cols[0] + norm_cols[1] + norm_cols[2] + norm_cols[3]
    norm_copies = [
        pltpu.make_async_remote_copy(
            norm.at[core, z], norm.at[core, z], nz_send.at[k], nz_recv.at[k], device_id=chip(k), device_id_type=MESH
        )
        for k in range(1, CHIPS)
    ]

    for copy in sum_copies:
        copy.wait_recv()
    total = chip_sums[0]
    for k in range(1, CHIPS):
        total = total + chip_sums[k]
    mine = total / D_MODEL
    factor[core] = mine
    fac = pltpu.make_async_remote_copy(
        factor.at[core], factor.at[core], fac_send, fac_recv, device_id=partner, device_id_type=MESH
    )
    fac.start()

    def piece(matrix, chip_at, core_at, d, part):
        at = (chip_at * CORES + core_at) * rows + d * half + part * size
        return out.at[matrix, pl.ds(pl.multiple_of(at, size), size)]

    def sign(d):
        return 1 if d == 0 else CHIPS - 1

    def across(d, s, j):
        matrix = core if j < PARTS else 1 - core
        ref = piece(matrix, lax.rem(z + (CHIPS - sign(d)) * s, CHIPS), core, d, j % PARTS)
        return pltpu.make_async_remote_copy(
            ref, ref, ici_send.at[d, s, j], ici_recv.at[d, s, j], device_id=chip(sign(d)), device_id_type=MESH
        )

    def over(d, b, j):
        matrix = core if j < PARTS else 1 - core
        ref = piece(matrix, lax.rem(z + (CHIPS - sign(d)) * b, CHIPS), core, d, j % PARTS)
        return pltpu.make_async_remote_copy(
            ref, ref, die_send.at[d, b, j], die_recv.at[d, b, j], device_id=partner, device_id_type=MESH
        )

    def scale(matrix, inverse, j):
        for d in range(2):
            at = d * half + (j % PARTS) * size
            base = pl.multiple_of(zero * rows + at, size)

            def body(i, _):
                fresh = held[matrix, 0, pl.ds(pl.multiple_of(at + i * 16, 16), 16)]
                out[matrix, pl.ds(pl.multiple_of(base + i * 16, 16), 16)] = (fresh * inverse).astype(jnp.bfloat16)
                return 0

            lax.fori_loop(0, size // 16, body, 0)

    inverse = 1.0 / mine
    for j in range(PARTS):
        scale(second, inverse, j)
        for d in range(2):
            across(d, 0, j).start()
            over(d, 0, j).start()
    for copy in norm_copies:
        copy.start()
    fac.wait_recv()
    inverse = 1.0 / factor[first]
    for j in range(PARTS, 2 * PARTS):
        scale(first, inverse, j)
        for d in range(2):
            across(d, 0, j).start()
            over(d, 0, j).start()

    for copy in norm_copies:
        copy.wait_recv()
    norm_pair = pltpu.make_async_remote_copy(
        norm.at[core], norm.at[core], np_send, np_recv, device_id=partner, device_id_type=MESH
    )
    norm_pair.start()

    def ring(s, _):
        for j in range(2 * PARTS):
            for d in range(2):
                across(d, s, j).wait_recv()

                @pl.when(s < CHIPS - 2)
                def _():
                    across(d, s + 1, j).start()

                over(d, s + 1, j).start()
        return 0

    lax.fori_loop(0, CHIPS - 1, ring, 0)

    pair.wait_send()
    fac.wait_send()
    norm_pair.wait()
    for copy in col_copies + sum_copies + norm_copies:
        copy.wait_send()

    def finish(s, _):
        for j in range(2 * PARTS):
            for d in range(2):
                across(d, s, j).wait_send()
                over(d, s, j).wait()
        return 0

    lax.fori_loop(0, CHIPS - 1, finish, 0)
    for j in range(2 * PARTS):
        for d in range(2):
            over(d, CHIPS - 1, j).wait()


def write_kernel(held, factor, norm, gate, up, factor_gate, factor_up, serve_norm, row, sems):
    copies = []
    pieces = 8
    step = gate.shape[0] // pieces
    for i in range(pieces):
        at = pl.ds(i * step, step)
        copies.append(pltpu.make_async_copy(held.at[0, at], gate.at[at], sems.at[0, i]))
        copies.append(pltpu.make_async_copy(held.at[1, at], up.at[at], sems.at[1, i]))
    copies.append(pltpu.make_async_copy(factor.at[0], factor_gate, sems.at[2, 0]))
    copies.append(pltpu.make_async_copy(factor.at[1], factor_up, sems.at[2, 1]))
    for copy in copies:
        copy.start()
    for i in range(CHIPS):
        for core in range(CORES):
            row[pl.ds(i * CORES + core, 1), :] = norm[core, i]
    serve_norm[...] = row[...].astype(jnp.bfloat16)
    for copy in copies:
        copy.wait()


def local(one_gate, other_gate, one_up, other_up, mix_share, norm_train, norm_step):
    rows, columns = one_gate.shape
    full = CHIPS * CORES * rows
    f32 = jnp.float32
    dma = pltpu.SemaphoreType.DMA
    vmem = pl.BlockSpec(memory_space=pltpu.VMEM)
    hbm = pl.BlockSpec(memory_space=pltpu.HBM)
    one_gate, other_gate, one_up, other_up = (
        pltpu.with_memory_space_constraint(a, pltpu.HBM) for a in (one_gate, other_gate, one_up, other_up)
    )
    held, factor, norm = pl.pallas_call(
        gather_kernel,
        name="gather",
        out_shape=(
            pltpu.VMEM((2, full, columns), jnp.bfloat16),
            pltpu.VMEM((2, 1, columns), f32),
            pltpu.VMEM((CORES, CHIPS, 1, 128), f32),
        ),
        in_specs=[hbm] * 4 + [vmem] * 3,
        out_specs=(vmem, vmem, vmem),
        scratch_shapes=[
            pltpu.VMEM((2, 2, rows, columns), f32),
            pltpu.VMEM((rows, rows), f32),
            pltpu.VMEM((2, 1, columns), f32),
            pltpu.VMEM((1, columns), f32),
            pltpu.VMEM((CHIPS, 1, columns), f32),
            pltpu.VMEM((COLS, 1, 128), f32),
            dma((2, 2, 4)),
            dma, dma,
            dma((CHIPS,)), dma((CHIPS,)),
            dma, dma,
            dma((COLS,)), dma((COLS,)),
            dma((CHIPS,)), dma((CHIPS,)),
            dma, dma,
            dma((2, CHIPS - 1, 2 * PARTS)), dma((2, CHIPS - 1, 2 * PARTS)),
            dma((2, CHIPS, 2 * PARTS)), dma((2, CHIPS, 2 * PARTS)),
        ],
        compiler_params=pltpu.CompilerParams(collective_id=0, has_side_effects=True, vmem_limit_bytes=8 * 2**20),
    )(one_gate, other_gate, one_up, other_up, mix_share.reshape(1, -1), norm_train.reshape(1, -1), norm_step.reshape(1, -1))
    held, factor, norm = (pltpu.with_memory_space_constraint(a, pltpu.VMEM) for a in (held, factor, norm))
    gate, up, factor_gate, factor_up, serve_norm = pl.pallas_call(
        write_kernel,
        name="write",
        out_shape=(
            jax.ShapeDtypeStruct((full, columns), jnp.bfloat16),
            jax.ShapeDtypeStruct((full, columns), jnp.bfloat16),
            jax.ShapeDtypeStruct((1, columns), f32),
            jax.ShapeDtypeStruct((1, columns), f32),
            jax.ShapeDtypeStruct((CHIPS * CORES, 128), jnp.bfloat16),
        ),
        in_specs=[vmem] * 3,
        out_specs=(hbm, hbm, hbm, hbm, vmem),
        scratch_shapes=[pltpu.VMEM((CHIPS * CORES, 128), f32), dma((3, 8))],
        compiler_params=pltpu.CompilerParams(vmem_limit_bytes=2 * 2**20),
    )(held, factor, norm)
    return gate, up, factor_gate.reshape(-1), factor_up.reshape(-1), serve_norm.reshape(-1)


def solution(mesh):
    return jax.shard_map(
        local,
        mesh=mesh,
        in_specs=(
            P(("ens", "zero"), "cols"),
            P(("ens", "zero"), "cols"),
            P(("ens", "zero"), "cols"),
            P(("ens", "zero"), "cols"),
            P(("ens", "zero")),
            P(("ens", "zero", "cols")),
            P(("ens", "zero", "cols")),
        ),
        out_specs=(
            P("ens", "cols"),
            P("ens", "cols"),
            P(("ens", "cols")),
            P(("ens", "cols")),
            P("ens"),
        ),
        check_vma=False,
    )
```

time: 148 us -> 108 us (0.73)
  Pallas kernels: 0 us -> 105 us
  waiting for transfers between devices: 76.9 us -> 0 us
  blocking collectives: 36.5 us -> 0 us
  between operations: 14.1 us -> 0.65 us
  local copies, waits for them, and re-layouts: 12.9 us -> 1.96 us
  other arithmetic: 7.51 us -> 0 us
    pallas_call x0 -> x2, Pallas kernels: none -> 105 us  [the longest x1 98.8 us: local(): pl.pallas_call(gather_kernel, name='gather', out_shape=(pltpu.VMEM((2, fu...]
    all_gather x1 -> x0, waiting for transfers between devices: 76.8 us -> none  [in_one_piece(): lax.all_gather(both, axis, axis=dim, tiled=True)]
    all_to_all x2 -> x0, blocking collectives: 36.5 us -> none  [from_everyone(): lax.all_to_all(jnp.broadcast_to(x[None], (size, *x.shape)), axis, 0, 0, t...]
    split x1 -> x0, local copies, waits for them, and re-layouts: 11.9 us -> none  [in_one_piece(): jnp.split(lax.all_gather(both, axis, axis=dim, tiled=True), ends, axis=al...]
    reduce_sum x2 -> x0, other arithmetic: 2.93 us -> none  [the longest x1 2.76 us: local(): jnp.sum(jnp.abs(fresh_gate), axis=0)]
    convert_element_type x2 -> x0, other arithmetic: 2.77 us -> none  [the longest x1 2.77 us: local(): (fresh_gate / factor_gate).astype(jnp.bfloat16)]
    unnamed x8 -> x6, local copies, waits for them, and re-layouts: 0.02 us -> 1.96 us
  transfers between devices with their start and end apart: 1 -> 0, of which waited for: 1 -> 0; matrix products, arithmetic and copies ran while one was open for 1% -> 0% of each run, Pallas kernels for 0% -> 0%
where the time goes in v1:
time: 108 us
  Pallas kernels  105 us (97%)
  local copies, waits for them, and re-layouts  1.96 us (2%)
    pallas_call x1, Pallas kernels, local(): pl.pallas_call(gather_kernel, name='gather', out_shape=(pltpu.VMEM((2, fu...  98.8 us
    pallas_call x1, Pallas kernels, local(): pl.pallas_call(write_kernel, name='write', out_shape=(jax.ShapeDtypeStruc...  6.63 us

profile of v1, /device:TPU:1, one launch (start us, length us, event | category | flops | bytes accessed | tf_op | source)
XLA Modules:
  0.0 108.1 jit_solution(4246579833251282702)
XLA Ops:
  0.6 0.0 copy-start
  0.6 0.6 copy-done
  1.3 0.0 copy-start.1
  1.3 0.7 copy-done.1
  1.9 0.0 copy-start.2
  1.9 0.7 copy-done.2
  2.6 98.8 %gather.1 = (bf16[2,2048,2048]{2,1,0:T(8,128)(2,1)S(1)}, f32[2,1,2048]{2,1,0:T(1,128)S(1)}, f32[2,8,1,128]{3,2,1,0:T(1,128)S(1)}) custom-call(f32[128,2048]{1,0:T(8,128)} %one_gate.1, f32[128,2048]{1,0:T(8,128)} %other_gate.1, f32[128,2048]{1,0:T(8,128)} %one_up.1, f32[128,2048]{1,0:T(8,128)} %other_up.1, f32[1,128]{1,0:T(1,128)S(1)} %bitcast.6, ...), custom_call_target="tpu_custom_call" | custom-call | tf_op jit(solution)/shard_map/gather/pallas_call | solution.py:260
  101.5 6.6 %write.1 = (bf16[2048,2048]{1,0:T(8,128)(2,1)}, bf16[2048,2048]{1,0:T(8,128)(2,1)}, f32[1,2048]{1,0:T(1,128)}, f32[1,2048]{1,0:T(1,128)}, bf16[16,128]{1,0:T(8,128)(2,1)}) custom-call(bf16[2,2048,2048]{2,1,0:T(8,128)(2,1)S(1)} %get-tuple-element.13.held, f32[2,1,2048]{2,1,0:T(1,128)S(1)} %get-tuple-element.14.factor, f32[2,8,1,128]{3,2,1,0:T(1,128)S(1)} %get-tuple-element.15.norm), custom_call_target="tpu_custom_call" | custom-call | tf_op jit(solution)/shard_map/write/pallas_call | solution.py:290
Async XLA Ops:
  0.6 0.7 copy-start
  1.3 0.7 copy-start.1
  1.9 0.7 copy-start.2

commit v2 on v1

--- a/solution.py
+++ b/solution.py
@@ -10,14 +10,14 @@
 CHIPS = 8
 CORES = 2
 COLS = 4
-PARTS = 2
+PARTS = 1
 
 
 def gather_kernel(
     one_gate, other_gate, one_up, other_up, mix, norm_train, norm_step,
     out, factor, norm,
-    held, mix_rows, sums, paired, chip_sums, norm_cols,
-    load_sem, pair_send, pair_recv, sum_send, sum_recv, fac_send, fac_recv,
+    held, mix_line, train_line, step_line, mix_rows, sums, paired, chip_sums, norm_cols,
+    load_sem, small_sem, pair_send, pair_recv, sum_send, sum_recv, fac_send, fac_recv,
     col_send, col_recv, nz_send, nz_recv, np_send, np_recv,
     ici_send, ici_recv, die_send, die_recv,
 ):
@@ -36,18 +36,25 @@
     def col(k):
         return {"cols": lax.rem(y + k, COLS)}
 
-    groups = 4
+    groups = 2
     step = rows // groups
 
     def load(matrix, which, g):
         source = ((one_gate, other_gate), (one_up, other_up))[matrix][which]
         at = pl.ds(g * step, step)
-        return pltpu.make_async_copy(source.at[at], held.at[matrix, which, at], load_sem.at[matrix, which, g])
+        return pltpu.make_async_copy(source.at[at], held.at[matrix, which, at], load_sem.at[matrix, g])
 
     def start_loads(matrix):
         for g in range(groups):
             for which in range(2):
                 load(matrix, which, g).start()
+
+    small = [
+        pltpu.make_async_copy(source, target, small_sem.at[i])
+        for i, (source, target) in enumerate(((mix, mix_line), (norm_train, train_line), (norm_step, step_line)))
+    ]
+    for copy in small:
+        copy.start()
 
     @pl.when(core == 0)
     def _():
@@ -66,19 +73,23 @@
     for k in range(1, COLS):
         pl.semaphore_signal(barrier, inc=1, device_id=col(k), device_id_type=MESH)
 
-    mix_rows[...] = jnp.broadcast_to(mix[...], (rows, rows)).T
+    for copy in small:
+        copy.wait()
+    mix_rows[...] = jnp.broadcast_to(mix_line[...], (rows, rows)).T
     lane = lax.broadcasted_iota(jnp.int32, (1, 128), 1)
-    gain = norm_train[...] + norm_step[...]
+    gain = train_line[...] + step_line[...]
     width = gain.shape[1]
     gain = jnp.concatenate([gain] * COLS, axis=1)
     norm_cols[y] = jnp.where((lane >= y * width) & (lane < (y + 1) * width), gain, 0.0)
 
+    def arrived(ref, sem):
+        pltpu.make_async_copy(ref, ref, sem).wait()
+
     def average(matrix):
         total = jnp.zeros((8, columns), jnp.float32)
         for g in range(groups):
-            for which in range(2):
-                at = pl.ds(g * step, step)
-                pltpu.make_async_copy(one_gate.at[at], held.at[matrix, which, at], load_sem.at[matrix, which, g]).wait()
+            landed = held.at[matrix, :, pl.ds(g * step, step)]
+            pltpu.make_async_copy(landed, landed, load_sem.at[matrix, g]).wait()
 
             def body(i, total):
                 at = pl.ds(pl.multiple_of(g * step + i * 8, 8), 8)
@@ -98,7 +109,7 @@
     pair.start()
     col_copies = [
         pltpu.make_async_remote_copy(
-            norm_cols.at[y], norm_cols.at[y], col_send.at[k], col_recv.at[k], device_id=col(k), device_id_type=MESH
+            norm_cols.at[y], norm_cols.at[y], col_send, col_recv, device_id=col(k), device_id_type=MESH
         )
         for k in range(1, COLS)
     ]
@@ -109,25 +120,23 @@
     chip_sums[z] = sums[second] + paired[...]
     sum_copies = [
         pltpu.make_async_remote_copy(
-            chip_sums.at[z], chip_sums.at[z], sum_send.at[k], sum_recv.at[k], device_id=chip(k), device_id_type=MESH
+            chip_sums.at[z], chip_sums.at[z], sum_send, sum_recv, device_id=chip(k), device_id_type=MESH
         )
         for k in (4, 3, 5, 2, 6, 1, 7)
     ]
     for copy in sum_copies:
         copy.start()
 
-    for copy in col_copies:
-        copy.wait_recv()
+    arrived(norm_cols.at[pl.ds(0, COLS - 1)], col_recv)
     norm[core, z] = norm_cols[0] + norm_cols[1] + norm_cols[2] + norm_cols[3]
     norm_copies = [
         pltpu.make_async_remote_copy(
-            norm.at[core, z], norm.at[core, z], nz_send.at[k], nz_recv.at[k], device_id=chip(k), device_id_type=MESH
+            norm.at[core, z], norm.at[core, z], nz_send, nz_recv, device_id=chip(k), device_id_type=MESH
         )
         for k in range(1, CHIPS)
     ]
 
-    for copy in sum_copies:
-        copy.wait_recv()
+    arrived(chip_sums.at[pl.ds(0, CHIPS - 1)], sum_recv)
     total = chip_sums[0]
     for k in range(1, CHIPS):
         total = total + chip_sums[k]
@@ -149,14 +158,14 @@
         matrix = core if j < PARTS else 1 - core
         ref = piece(matrix, lax.rem(z + (CHIPS - sign(d)) * s, CHIPS), core, d, j % PARTS)
         return pltpu.make_async_remote_copy(
-            ref, ref, ici_send.at[d, s, j], ici_recv.at[d, s, j], device_id=chip(sign(d)), device_id_type=MESH
+            ref, ref, ici_send, ici_recv.at[d, s, j], device_id=chip(sign(d)), device_id_type=MESH
         )
 
     def over(d, b, j):
         matrix = core if j < PARTS else 1 - core
         ref = piece(matrix, lax.rem(z + (CHIPS - sign(d)) * b, CHIPS), core, d, j % PARTS)
         return pltpu.make_async_remote_copy(
-            ref, ref, die_send.at[d, b, j], die_recv.at[d, b, j], device_id=partner, device_id_type=MESH
+            ref, ref, die_send, die_recv, device_id=partner, device_id_type=MESH
         )
 
     def scale(matrix, inverse, j):
@@ -187,8 +196,7 @@
             across(d, 0, j).start()
             over(d, 0, j).start()
 
-    for copy in norm_copies:
-        copy.wait_recv()
+    arrived(norm.at[core, pl.ds(0, CHIPS - 1)], nz_recv)
     norm_pair = pltpu.make_async_remote_copy(
         norm.at[core], norm.at[core], np_send, np_recv, device_id=partner, device_id_type=MESH
     )
@@ -211,40 +219,38 @@
     pair.wait_send()
     fac.wait_send()
     norm_pair.wait()
-    for copy in col_copies + sum_copies + norm_copies:
-        copy.wait_send()
-
-    def finish(s, _):
-        for j in range(2 * PARTS):
-            for d in range(2):
-                across(d, s, j).wait_send()
-                over(d, s, j).wait()
-        return 0
-
-    lax.fori_loop(0, CHIPS - 1, finish, 0)
-    for j in range(2 * PARTS):
-        for d in range(2):
-            over(d, CHIPS - 1, j).wait()
-
-
-def write_kernel(held, factor, norm, gate, up, factor_gate, factor_up, serve_norm, row, sems):
-    copies = []
-    pieces = 8
+    arrived(norm_cols.at[pl.ds(0, COLS - 1)], col_send)
+    arrived(chip_sums.at[pl.ds(0, CHIPS - 1)], sum_send)
+    arrived(norm.at[core, pl.ds(0, CHIPS - 1)], nz_send)
+    arrived(out.at[0, pl.ds(0, 2 * (CHIPS - 1) * rows)], ici_send)
+    arrived(out.at[0], die_send)
+    arrived(out.at[0], die_recv)
+
+
+def write_kernel(held, factor, norm, gate, up, factor_gate, factor_up, serve_norm, row, line, sems):
+    pieces = 16
     step = gate.shape[0] // pieces
     for i in range(pieces):
-        at = pl.ds(i * step, step)
-        copies.append(pltpu.make_async_copy(held.at[0, at], gate.at[at], sems.at[0, i]))
-        copies.append(pltpu.make_async_copy(held.at[1, at], up.at[at], sems.at[1, i]))
-    copies.append(pltpu.make_async_copy(factor.at[0], factor_gate, sems.at[2, 0]))
-    copies.append(pltpu.make_async_copy(factor.at[1], factor_up, sems.at[2, 1]))
-    for copy in copies:
+        for matrix, target in enumerate((gate, up)):
+            at = pl.ds(i * step, step)
+            pltpu.make_async_copy(held.at[matrix, at], target.at[at], sems.at[matrix]).start()
+    factors = [
+        pltpu.make_async_copy(factor.at[matrix], target, sems.at[2 + matrix])
+        for matrix, target in enumerate((factor_gate, factor_up))
+    ]
+    for copy in factors:
         copy.start()
     for i in range(CHIPS):
         for core in range(CORES):
             row[pl.ds(i * CORES + core, 1), :] = norm[core, i]
-    serve_norm[...] = row[...].astype(jnp.bfloat16)
-    for copy in copies:
+    line[...] = row[...].astype(jnp.bfloat16)
+    last = pltpu.make_async_copy(line, serve_norm, sems.at[4])
+    last.start()
+    for copy in factors:
         copy.wait()
+    for matrix, target in enumerate((gate, up)):
+        pltpu.make_async_copy(held.at[matrix], target, sems.at[matrix]).wait()
+    last.wait()
 
 
 def local(one_gate, other_gate, one_up, other_up, mix_share, norm_train, norm_step):
@@ -254,9 +260,13 @@
     dma = pltpu.SemaphoreType.DMA
     vmem = pl.BlockSpec(memory_space=pltpu.VMEM)
     hbm = pl.BlockSpec(memory_space=pltpu.HBM)
-    one_gate, other_gate, one_up, other_up = (
-        pltpu.with_memory_space_constraint(a, pltpu.HBM) for a in (one_gate, other_gate, one_up, other_up)
-    )
+    taken = [
+        pltpu.with_memory_space_constraint(a, pltpu.HBM)
+        for a in (
+            one_gate, other_gate, one_up, other_up,
+            mix_share.reshape(1, -1), norm_train.reshape(1, -1), norm_step.reshape(1, -1),
+        )
+    ]
     held, factor, norm = pl.pallas_call(
         gather_kernel,
         name="gather",
@@ -265,27 +275,25 @@
             pltpu.VMEM((2, 1, columns), f32),
             pltpu.VMEM((CORES, CHIPS, 1, 128), f32),
         ),
-        in_specs=[hbm] * 4 + [vmem] * 3,
+        in_specs=[hbm] * 7,
         out_specs=(vmem, vmem, vmem),
         scratch_shapes=[
             pltpu.VMEM((2, 2, rows, columns), f32),
+            pltpu.VMEM((1, rows), f32),
+            pltpu.VMEM((1, norm_train.size), f32),
+            pltpu.VMEM((1, norm_train.size), f32),
             pltpu.VMEM((rows, rows), f32),
             pltpu.VMEM((2, 1, columns), f32),
             pltpu.VMEM((1, columns), f32),
             pltpu.VMEM((CHIPS, 1, columns), f32),
             pltpu.VMEM((COLS, 1, 128), f32),
-            dma((2, 2, 4)),
-            dma, dma,
-            dma((CHIPS,)), dma((CHIPS,)),
-            dma, dma,
-            dma((COLS,)), dma((COLS,)),
-            dma((CHIPS,)), dma((CHIPS,)),
-            dma, dma,
-            dma((2, CHIPS - 1, 2 * PARTS)), dma((2, CHIPS - 1, 2 * PARTS)),
-            dma((2, CHIPS, 2 * PARTS)), dma((2, CHIPS, 2 * PARTS)),
+            dma((2, 2)), dma((3,)),
+            dma, dma, dma, dma, dma, dma,
+            dma, dma, dma, dma, dma, dma,
+            dma, dma((2, CHIPS - 1, 2 * PARTS)), dma, dma,
         ],
         compiler_params=pltpu.CompilerParams(collective_id=0, has_side_effects=True, vmem_limit_bytes=8 * 2**20),
-    )(one_gate, other_gate, one_up, other_up, mix_share.reshape(1, -1), norm_train.reshape(1, -1), norm_step.reshape(1, -1))
+    )(*taken)
     held, factor, norm = (pltpu.with_memory_space_constraint(a, pltpu.VMEM) for a in (held, factor, norm))
     gate, up, factor_gate, factor_up, serve_norm = pl.pallas_call(
         write_kernel,
@@ -298,8 +306,8 @@
             jax.ShapeDtypeStruct((CHIPS * CORES, 128), jnp.bfloat16),
         ),
         in_specs=[vmem] * 3,
-        out_specs=(hbm, hbm, hbm, hbm, vmem),
-        scratch_shapes=[pltpu.VMEM((CHIPS * CORES, 128), f32), dma((3, 8))],
+        out_specs=(hbm,) * 5,
+        scratch_shapes=[pltpu.VMEM((CHIPS * CORES, 128), f32), pltpu.VMEM((CHIPS * CORES, 128), jnp.bfloat16), dma((5,))],
         compiler_params=pltpu.CompilerParams(vmem_limit_bytes=2 * 2**20),
     )(held, factor, norm)
     return gate, up, factor_gate.reshape(-1), factor_up.reshape(-1), serve_norm.reshape(-1)

time: 108 us -> 104 us (0.963)
  Pallas kernels: 105 us -> 103 us
  local copies, waits for them, and re-layouts: 1.96 us -> 0 us
    unnamed x6 -> x0, local copies, waits for them, and re-layouts: 1.96 us -> none
    pallas_call x1, Pallas kernels: 98.8 us -> 97.2 us  [local(): pl.pallas_call(gather_kernel, name='gather', out_shape=(pltpu.VMEM((2, fu...]
where the time goes in v2:
time: 104 us
  Pallas kernels  103 us (99%)
    pallas_call x1, Pallas kernels, local(): pl.pallas_call(gather_kernel, name='gather', out_shape=(pltpu.VMEM((2, fu...  97.2 us
    pallas_call x1, Pallas kernels, local(): pl.pallas_call(write_kernel, name='write', out_shape=(jax.ShapeDtypeStruc...  5.84 us

profile of v2, /device:TPU:1, one launch (start us, length us, event | category | flops | bytes accessed | tf_op | source)
XLA Modules:
  0.0 103.6 jit_solution(7270682608637165805)
XLA Ops:
  0.6 97.2 %gather.1 = (bf16[2,2048,2048]{2,1,0:T(8,128)(2,1)S(1)}, f32[2,1,2048]{2,1,0:T(1,128)S(1)}, f32[2,8,1,128]{3,2,1,0:T(1,128)S(1)}) custom-call(f32[128,2048]{1,0:T(8,128)} %one_gate.1, f32[128,2048]{1,0:T(8,128)} %other_gate.1, f32[128,2048]{1,0:T(8,128)} %one_up.1, f32[128,2048]{1,0:T(8,128)} %other_up.1, f32[1,128]{1,0:T(1,128)} %bitcast.6, ...), custom_call_target="tpu_custom_call" | custom-call | tf_op jit(solution)/shard_map/gather/pallas_call | solution.py:270
  97.8 5.8 %write.1 = (bf16[2048,2048]{1,0:T(8,128)(2,1)}, bf16[2048,2048]{1,0:T(8,128)(2,1)}, f32[1,2048]{1,0:T(1,128)}, f32[1,2048]{1,0:T(1,128)}, bf16[16,128]{1,0:T(8,128)(2,1)}) custom-call(bf16[2,2048,2048]{2,1,0:T(8,128)(2,1)S(1)} %get-tuple-element.13.held, f32[2,1,2048]{2,1,0:T(1,128)S(1)} %get-tuple-element.14.factor, f32[2,8,1,128]{3,2,1,0:T(1,128)S(1)} %get-tuple-element.15.norm), custom_call_target="tpu_custom_call" | custom-call | tf_op jit(solution)/shard_map/write/pallas_call | solution.py:298

commit v3 on v2

--- a/solution.py
+++ b/solution.py
@@ -10,16 +10,17 @@
 CHIPS = 8
 CORES = 2
 COLS = 4
-PARTS = 1
+PARTS = 2
+EARLY = (8, 16)
 
 
 def gather_kernel(
     one_gate, other_gate, one_up, other_up, mix, norm_train, norm_step,
     out, factor, norm,
-    held, mix_line, train_line, step_line, mix_rows, sums, paired, chip_sums, norm_cols,
+    held, early, mix_line, train_line, step_line, mix_rows, sums, paired, chip_sums, norm_cols,
     load_sem, small_sem, pair_send, pair_recv, sum_send, sum_recv, fac_send, fac_recv,
     col_send, col_recv, nz_send, nz_recv, np_send, np_recv,
-    ici_send, ici_recv, die_send, die_recv,
+    early_send, early_recv, ici_send, ici_recv, die_send, die_recv,
 ):
     zero = lax.axis_index("zero")
     y = lax.axis_index("cols")
@@ -33,6 +34,9 @@
     def chip(k):
         return {"zero": lax.rem(z + k, CHIPS) * CORES + core}
 
+    def sign(d):
+        return 1 if d == 0 else CHIPS - 1
+
     def col(k):
         return {"cols": lax.rem(y + k, COLS)}
 
@@ -115,6 +119,22 @@
     ]
     for copy in col_copies:
         copy.start()
+
+    def ahead(i, d):
+        start = (0, EARLY[0])[i]
+        at = pl.ds(d * half + start, EARLY[i] - start)
+        return pltpu.make_async_remote_copy(
+            held.at[first, 0, at],
+            early.at[d, pl.ds(start, EARLY[i] - start)],
+            early_send,
+            early_recv,
+            device_id=chip(sign(d)),
+            device_id_type=MESH,
+        )
+
+    if EARLY[0]:
+        for d in range(2):
+            ahead(0, d).start()
     average(second)
     pair.wait_recv()
     chip_sums[z] = sums[second] + paired[...]
@@ -126,6 +146,9 @@
     ]
     for copy in sum_copies:
         copy.start()
+    if EARLY[1] > EARLY[0]:
+        for d in range(2):
+            ahead(1, d).start()
 
     arrived(norm_cols.at[pl.ds(0, COLS - 1)], col_recv)
     norm[core, z] = norm_cols[0] + norm_cols[1] + norm_cols[2] + norm_cols[3]
@@ -151,12 +174,11 @@
         at = (chip_at * CORES + core_at) * rows + d * half + part * size
         return out.at[matrix, pl.ds(pl.multiple_of(at, size), size)]
 
-    def sign(d):
-        return 1 if d == 0 else CHIPS - 1
-
-    def across(d, s, j):
+    def across(d, s, j, skip=0):
         matrix = core if j < PARTS else 1 - core
         ref = piece(matrix, lax.rem(z + (CHIPS - sign(d)) * s, CHIPS), core, d, j % PARTS)
+        if skip:
+            ref = ref.at[pl.ds(skip, size - skip)]
         return pltpu.make_async_remote_copy(
             ref, ref, ici_send, ici_recv.at[d, s, j], device_id=chip(sign(d)), device_id_type=MESH
         )
@@ -168,17 +190,18 @@
             ref, ref, die_send, die_recv, device_id=partner, device_id_type=MESH
         )
 
+    def narrow(source, target, count, inverse):
+        def body(i, _):
+            at = pl.ds(pl.multiple_of(i * 8, 8), 8)
+            target[at] = (source[at] * inverse).astype(jnp.bfloat16)
+            return 0
+
+        lax.fori_loop(0, count // 8, body, 0)
+
     def scale(matrix, inverse, j):
         for d in range(2):
-            at = d * half + (j % PARTS) * size
-            base = pl.multiple_of(zero * rows + at, size)
-
-            def body(i, _):
-                fresh = held[matrix, 0, pl.ds(pl.multiple_of(at + i * 16, 16), 16)]
-                out[matrix, pl.ds(pl.multiple_of(base + i * 16, 16), 16)] = (fresh * inverse).astype(jnp.bfloat16)
-                return 0
-
-            lax.fori_loop(0, size // 16, body, 0)
+            at = pl.ds(d * half + (j % PARTS) * size, size)
+            narrow(held.at[matrix, 0, at], piece(matrix, z, core, d, j % PARTS), size, inverse)
 
     inverse = 1.0 / mine
     for j in range(PARTS):
@@ -193,8 +216,11 @@
     for j in range(PARTS, 2 * PARTS):
         scale(first, inverse, j)
         for d in range(2):
-            across(d, 0, j).start()
+            across(d, 0, j, EARLY[1] if j == PARTS else 0).start()
             over(d, 0, j).start()
+    arrived(early.at[:, pl.ds(0, EARLY[1])], early_recv)
+    for d in range(2):
+        narrow(early.at[d], piece(first, lax.rem(z + CHIPS - sign(d), CHIPS), core, d, 0), EARLY[1], inverse)
 
     arrived(norm.at[core, pl.ds(0, CHIPS - 1)], nz_recv)
     norm_pair = pltpu.make_async_remote_copy(
@@ -202,10 +228,10 @@
     )
     norm_pair.start()
 
-    def ring(s, _):
+    def ring(s, _, first_step=False):
         for j in range(2 * PARTS):
             for d in range(2):
-                across(d, s, j).wait_recv()
+                across(d, s, j, EARLY[1] if first_step and j == PARTS else 0).wait_recv()
 
                 @pl.when(s < CHIPS - 2)
                 def _():
@@ -214,7 +240,8 @@
                 over(d, s + 1, j).start()
         return 0
 
-    lax.fori_loop(0, CHIPS - 1, ring, 0)
+    ring(0, 0, True)
+    lax.fori_loop(1, CHIPS - 1, ring, 0)
 
     pair.wait_send()
     fac.wait_send()
@@ -222,7 +249,8 @@
     arrived(norm_cols.at[pl.ds(0, COLS - 1)], col_send)
     arrived(chip_sums.at[pl.ds(0, CHIPS - 1)], sum_send)
     arrived(norm.at[core, pl.ds(0, CHIPS - 1)], nz_send)
-    arrived(out.at[0, pl.ds(0, 2 * (CHIPS - 1) * rows)], ici_send)
+    arrived(early.at[:, pl.ds(0, EARLY[1])], early_send)
+    arrived(out.at[0, pl.ds(0, 2 * (CHIPS - 1) * rows - 2 * EARLY[1])], ici_send)
     arrived(out.at[0], die_send)
     arrived(out.at[0], die_recv)
 
@@ -279,6 +307,7 @@
         out_specs=(vmem, vmem, vmem),
         scratch_shapes=[
             pltpu.VMEM((2, 2, rows, columns), f32),
+            pltpu.VMEM((2, rows // 4, columns), f32),
             pltpu.VMEM((1, rows), f32),
             pltpu.VMEM((1, norm_train.size), f32),
             pltpu.VMEM((1, norm_train.size), f32),
@@ -290,7 +319,7 @@
             dma((2, 2)), dma((3,)),
             dma, dma, dma, dma, dma, dma,
             dma, dma, dma, dma, dma, dma,
-            dma, dma((2, CHIPS - 1, 2 * PARTS)), dma, dma,
+            dma, dma, dma, dma((2, CHIPS - 1, 2 * PARTS)), dma, dma,
         ],
         compiler_params=pltpu.CompilerParams(collective_id=0, has_side_effects=True, vmem_limit_bytes=8 * 2**20),
     )(*taken)

time: 104 us -> 102 us (0.981)
  Pallas kernels: 103 us -> 101 us
    pallas_call x1, Pallas kernels: 97.2 us -> 95.6 us  [local(): pl.pallas_call(gather_kernel, name='gather', out_shape=(pltpu.VMEM((2, fu...]
where the time goes in v3:
time: 102 us
  Pallas kernels  101 us (99%)
    pallas_call x1, Pallas kernels, local(): pl.pallas_call(gather_kernel, name='gather', out_shape=(pltpu.VMEM((2, fu...  95.6 us
    pallas_call x1, Pallas kernels, local(): pl.pallas_call(write_kernel, name='write', out_shape=(jax.ShapeDtypeStruc...  5.84 us

profile of v3, /device:TPU:1, one launch (start us, length us, event | category | flops | bytes accessed | tf_op | source)
XLA Modules:
  0.0 102.1 jit_solution(8053065501430567584)
XLA Ops:
  0.6 95.6 %gather.1 = (bf16[2,2048,2048]{2,1,0:T(8,128)(2,1)S(1)}, f32[2,1,2048]{2,1,0:T(1,128)S(1)}, f32[2,8,1,128]{3,2,1,0:T(1,128)S(1)}) custom-call(f32[128,2048]{1,0:T(8,128)} %one_gate.1, f32[128,2048]{1,0:T(8,128)} %other_gate.1, f32[128,2048]{1,0:T(8,128)} %one_up.1, f32[128,2048]{1,0:T(8,128)} %other_up.1, f32[1,128]{1,0:T(1,128)} %bitcast.6, ...), custom_call_target="tpu_custom_call" | custom-call | tf_op jit(solution)/shard_map/gather/pallas_call | solution.py:298
  96.2 5.8 %write.1 = (bf16[2048,2048]{1,0:T(8,128)(2,1)}, bf16[2048,2048]{1,0:T(8,128)(2,1)}, f32[1,2048]{1,0:T(1,128)}, f32[1,2048]{1,0:T(1,128)}, bf16[16,128]{1,0:T(8,128)(2,1)}) custom-call(bf16[2,2048,2048]{2,1,0:T(8,128)(2,1)S(1)} %get-tuple-element.13.held, f32[2,1,2048]{2,1,0:T(1,128)S(1)} %get-tuple-element.14.factor, f32[2,8,1,128]{3,2,1,0:T(1,128)S(1)} %get-tuple-element.15.norm), custom_call_target="tpu_custom_call" | custom-call | tf_op jit(solution)/shard_map/write/pallas_call | solution.py:327
